TPU v7x, 256 devices: a whole 4x4x8 slice. The times are simulated.
256 devices in a mesh: batch: 2 (over y_lo), space: 64 (over x, y_hi, z), hidden: 2 (over core).
Axes of the slice: x: 4, y: 4 (y_hi: 2, y_lo: 2; y = y_hi * 2 + y_lo), z: 8, core: 2. Of those that a mesh axis runs over, the one named last changes fastest.
Arguments:
- nodes: bfloat16 [2, 8192, 512], P('batch', 'space'), may hold values from -6 to 6
- edges: bfloat16 [2, 65536, 512], P('batch', 'space'), may hold values from -6 to 6
- node_cotangent: bfloat16 [2, 8192, 512], P('batch', 'space'), may hold values from -18 to 18
- edge_cotangent: bfloat16 [2, 65536, 512], P('batch', 'space'), may hold values from -18 to 18
- senders: int32 [65536], P('space'), may hold values from 0 to 255
- receivers: int32 [65536], P('space'), may hold values from 0 to 127
- send_lists: int32 [64, 2, 64], P('space'), may hold values from 0 to 127
- edge_first: bfloat16 [1536, 512], P(None, 'hidden'), may hold values from -0.15625 to 0.15625
- edge_bias: float32 [512], P('hidden'), may hold values from -3 to 3
- edge_second: bfloat16 [512, 512], P('hidden'), may hold values from -0.25 to 0.25
- edge_gain: float32 [512], replicated, may hold values from 0.1 to 1.9
- node_first: bfloat16 [1024, 512], replicated, may hold values from -0.1875 to 0.1875
- node_bias: float32 [512], replicated, may hold values from -3 to 3
- node_second: bfloat16 [512, 512], replicated, may hold values from -0.25 to 0.25
- node_gain: float32 [512], replicated, may hold values from 0.1 to 1.9
Outputs:
- grad_nodes: bfloat16 [2, 8192, 512], P('batch', 'space', 'hidden')
- grad_edges: bfloat16 [2, 65536, 512], P('batch', 'space', 'hidden')
- grad_edge_first: float32 [1536, 512], P(None, 'hidden')
- grad_edge_bias: float32 [512], P('hidden')
- grad_edge_second: float32 [512, 512], P('hidden')
- grad_edge_gain: float32 [512], replicated
- grad_node_first: float32 [1024, 512], replicated
- grad_node_bias: float32 [512], replicated
- grad_node_second: float32 [512, 512], replicated
- grad_node_gain: float32 [512], replicated
Inputs may be any that keep to these rules, and one draw needn't show every extreme that they name: `senders`: an entry below 128 is a local node of the edge's patch; 128 + k is row k of the previous patch's list 1, 192 + k row k of the next patch's list 0. `receivers`: local nodes of the edge's patch. `send_lists`: local nodes of the patch; entries may repeat.
All inputs are finite; a program needn't handle non-finite values.
Results may differ from a plain program's by a relative error of at most 0.015.
Values may be sent and summed in bfloat16 or wider, within the bound.
A program may use at most 128 MiB of HBM per device.

v0:
```python
import jax
import jax.numpy as jnp
from jax import lax
from jax.sharding import PartitionSpec as P

EPS = 1e-05


def extended(cells, sides, width):
    for axis, dim in sides:
        count = lax.axis_size(axis)
        head = lax.slice_in_dim(cells, 0, width, axis=dim)
        tail = lax.slice_in_dim(cells, cells.shape[dim] - width, cells.shape[dim], axis=dim)
        cells = jnp.concatenate(
            [
                lax.ppermute(tail, axis, [(i, (i + 1) % count) for i in range(count)]),
                cells,
                lax.ppermute(head, axis, [((i + 1) % count, i) for i in range(count)]),
            ],
            axis=dim,
        )
    return cells


def copy_for_each(value, axis):
    devices = lax.axis_size(axis)
    return lax.all_to_all(
        jnp.broadcast_to(value[None], (devices, *value.shape)), axis, 0, 0, tiled=True
    )


def taken_together(value, axis):
    return copy_for_each(value, axis).astype(jnp.float32).sum(axis=0)


def cut_along(value, dim, devices):
    lengths = value.shape
    pieces = value.reshape(*lengths[:dim], devices, lengths[dim] // devices, *lengths[dim + 1 :])
    return jnp.moveaxis(pieces, dim, 0)


def sent_and_summed(value, axis, dim):
    devices = lax.axis_size(axis)
    pieces = lax.all_to_all(cut_along(value, dim, devices), axis, 0, 0, tiled=True)
    return jnp.sum(pieces.astype(jnp.float32), axis=0)


def in_one_piece(arrays, axis, dim, along):
    ends, at = ([], 0)
    for a in arrays[:-1]:
        at += a.shape[along]
        ends.append(at)
    both = jnp.concatenate(arrays, axis=along)
    return tuple(jnp.split(sent_and_summed(both, axis, dim), ends, axis=along))


def in_one(arrays, axis):
    ends = [0]
    for a in arrays:
        ends.append(ends[-1] + a.size)
    so_far = lax.psum(jnp.concatenate([a.ravel() for a in arrays]), axis)
    return tuple((so_far[b:e].reshape(a.shape) for a, b, e in zip(arrays, ends, ends[1:])))


def one_hot(indices, columns, wanted):
    return (indices[:, None] == jnp.arange(columns, dtype=jnp.int32)[None, :]).astype(wanted)


def matmul(lefthand, righthand):
    return jnp.dot(lefthand, righthand, preferred_element_type=jnp.float32)


def matmul_tn(lefthand, righthand):
    return lax.dot_general(
        lefthand, righthand, (((0,), (0,)), ((), ())), preferred_element_type=jnp.float32
    )


def matmul_nt(lefthand, righthand):
    return lax.dot_general(
        lefthand, righthand, (((1,), (1,)), ((), ())), preferred_element_type=jnp.float32
    )


def exact_tn(lefthand, righthand):
    return lax.dot_general(
        lefthand,
        righthand,
        (((0,), (0,)), ((), ())),
        precision=lax.Precision.HIGHEST,
        preferred_element_type=jnp.float32,
    )


def normalize(values):
    centre = values - jnp.mean(values, axis=-1, keepdims=True)
    scaled = lax.rsqrt(jnp.mean(centre * centre, axis=-1, keepdims=True) + EPS)
    return (centre * scaled, scaled)


def norm_back(upstream, gain_vec, normed, scaled):
    pulled = upstream * gain_vec
    return scaled * (
        pulled
        - jnp.mean(pulled, axis=-1, keepdims=True)
        - normed * jnp.mean(pulled * normed, axis=-1, keepdims=True)
    )


def silu_slope(values):
    logistic = jax.nn.sigmoid(values)
    return logistic * (1.0 + values * (1.0 - logistic))


def on_device(
    nodes,
    edges,
    node_cotangent,
    edge_cotangent,
    senders,
    receivers,
    send_lists,
    edge_first,
    edge_bias,
    edge_second,
    edge_gain,
    node_first,
    node_bias,
    node_second,
    node_gain,
):
    splits = lax.axis_size("hidden")
    my_part = lax.axis_index("hidden")
    width = nodes.shape[2]
    half = width // splits
    node_rows = nodes[0]
    node_count = node_rows.shape[0]
    halo_count = send_lists.shape[2]
    listed = send_lists[0].reshape(-1)
    picker = one_hot(listed, node_count, jnp.bfloat16)
    outgoing = matmul(picker, node_rows).astype(jnp.bfloat16).reshape(2, halo_count, width)
    padded = extended(outgoing, (("space", 0),), 1)
    table = jnp.concatenate([node_rows, padded[0], padded[3]], axis=0)
    table_rows = table.shape[0]
    sender_hot = one_hot(senders, table_rows, jnp.bfloat16)
    receiver_hot = one_hot(receivers, node_count, jnp.bfloat16)
    from_sender = matmul(sender_hot, table).astype(jnp.bfloat16)
    from_receiver = matmul(receiver_hot, node_rows).astype(jnp.bfloat16)
    edge_input = jnp.concatenate([edges[0], from_sender, from_receiver], axis=1)
    edge_pre = matmul(edge_input, edge_first) + edge_bias
    edge_act = jax.nn.silu(edge_pre).astype(jnp.bfloat16)
    edge_total = taken_together(
        matmul(edge_act, edge_second).astype(jnp.bfloat16), "hidden"
    ).astype(jnp.float32)
    edge_normed, edge_scale = normalize(edge_total)
    message = (edge_gain * edge_normed).astype(jnp.bfloat16)
    gathered = matmul_tn(receiver_hot, message).astype(jnp.bfloat16)
    node_input = jnp.concatenate([node_rows, gathered], axis=1)
    node_pre = matmul(node_input, node_first) + node_bias
    node_act = jax.nn.silu(node_pre).astype(jnp.bfloat16)
    node_normed, node_scale = normalize(matmul(node_act, node_second))
    node_upstream = node_cotangent[0].astype(jnp.float32)
    node_gain_grad = jnp.sum(node_upstream * node_normed, axis=0)
    node_dz = norm_back(node_upstream, node_gain, node_normed, node_scale).astype(jnp.bfloat16)
    node_second_grad = matmul_tn(node_act, node_dz)
    node_dh = (matmul_nt(node_dz, node_second) * silu_slope(node_pre)).astype(jnp.bfloat16)
    node_first_grad = matmul_tn(node_input, node_dh)
    node_bias_grad = jnp.sum(node_dh.astype(jnp.float32), axis=0)
    node_dx = matmul_nt(node_dh, node_first)
    agg_grad = node_dx[:, width:].astype(jnp.bfloat16)
    edge_upstream = edge_cotangent[0].astype(jnp.float32)
    message_grad = edge_upstream + matmul(receiver_hot, agg_grad)
    edge_gain_grad = jnp.sum(message_grad * edge_normed, axis=0)
    edge_dz = norm_back(message_grad, edge_gain, edge_normed, edge_scale).astype(jnp.bfloat16)
    edge_second_grad = matmul_tn(edge_act, edge_dz)
    edge_dh = (matmul_nt(edge_dz, edge_second) * silu_slope(edge_pre)).astype(jnp.bfloat16)
    edge_first_grad = matmul_tn(edge_input, edge_dh)
    edge_bias_grad = jnp.sum(edge_dh.astype(jnp.float32), axis=0)
    sender_exact = one_hot(senders, table_rows, jnp.float32)
    receiver_exact = one_hot(receivers, node_count, jnp.float32)
    partial_grad = matmul_nt(edge_dh, edge_first)
    sender_part = exact_tn(sender_exact, partial_grad[:, width : 2 * width])
    receiver_part = exact_tn(receiver_exact, partial_grad[:, 2 * width :])
    table_part = jnp.concatenate(
        [sender_part[:node_count] + receiver_part, sender_part[node_count:]], axis=0
    )
    edge_own, table_grad = in_one_piece(
        (partial_grad[:, :width].astype(jnp.bfloat16), table_part.astype(jnp.bfloat16)),
        "hidden",
        1,
        0,
    )
    returning = jnp.stack(
        [table_grad[node_count : node_count + halo_count], table_grad[node_count + halo_count :]],
        axis=0,
    )
    returned = extended(returning.astype(jnp.bfloat16), (("space", 0),), 1).astype(returning.dtype)
    arriving = jnp.concatenate([returned[0], returned[3]], axis=0)
    halo_grad = exact_tn(one_hot(listed, node_count, jnp.float32), arriving)
    own_cot = lax.dynamic_slice_in_dim(node_upstream, my_part * half, half, 1)
    own_node = lax.dynamic_slice_in_dim(node_dx, my_part * half, half, 1)
    grad_nodes = (own_cot + own_node + table_grad[:node_count] + halo_grad).astype(jnp.bfloat16)[
        None
    ]
    own_edge_cot = lax.dynamic_slice_in_dim(edge_upstream, my_part * half, half, 1)
    grad_edges = (own_edge_cot + edge_own).astype(jnp.bfloat16)[None]
    (
        edge_first_grad,
        edge_bias_grad,
        edge_second_grad,
        edge_gain_grad,
        node_first_grad,
        node_bias_grad,
        node_second_grad,
        node_gain_grad,
    ) = tuple(
        (
            part.astype(jnp.float32)
            for part in in_one(
                (
                    edge_first_grad.astype(jnp.bfloat16),
                    edge_bias_grad.astype(jnp.bfloat16),
                    edge_second_grad.astype(jnp.bfloat16),
                    edge_gain_grad.astype(jnp.bfloat16),
                    node_first_grad.astype(jnp.bfloat16),
                    node_bias_grad.astype(jnp.bfloat16),
                    node_second_grad.astype(jnp.bfloat16),
                    node_gain_grad.astype(jnp.bfloat16),
                ),
                ("batch", "space"),
            )
        )
    )
    return (
        grad_nodes,
        grad_edges,
        edge_first_grad,
        edge_bias_grad,
        edge_second_grad,
        edge_gain_grad,
        node_first_grad,
        node_bias_grad,
        node_second_grad,
        node_gain_grad,
    )


def solution(mesh):
    placed = (
        P("batch", "space", None),
        P("batch", "space", None),
        P("batch", "space", None),
        P("batch", "space", None),
        P("space"),
        P("space"),
        P("space", None, None),
        P(None, "hidden"),
        P("hidden"),
        P("hidden", None),
        P(),
        P(),
        P(),
        P(),
        P(),
    )
    return jax.shard_map(
        on_device,
        mesh=mesh,
        in_specs=placed,
        out_specs=(
            P("batch", "space", "hidden"),
            P("batch", "space", "hidden"),
            P(None, "hidden"),
            P("hidden"),
            P("hidden", None),
            P(),
            P(),
            P(),
            P(),
            P(),
        ),
        check_vma=False,
    )
```

profile of v0, /device:TPU:2, one launch (start us, length us, event | category | flops | bytes accessed | tf_op | source)
XLA Modules:
  0.0 336.3 jit_solution(7981863708176337390)
XLA Ops:
  7.2 0.9 eq.26
  8.1 1.1 convolution_convert_fusion.8
  9.3 2.0 collective-permute-start
  11.3 6.6 %collective-permute-start.1 = (bf16[1,64,512]{2,1,0:T(8,128)(2,1)S(1)}, bf16[1,64,512]{2,1,0:T(8,128)(2,1)S(1)}, u32[]{:S(2)}, u32[]{:S(2)}) collective-permute-start(bf16[1,64,512]{2,1,0:T(8,128)(2,1)S(1)} %get-tuple-element.26), channel_id=1, source_target_pairs={{2,0},{4,2},{6,4},{8,6},{10,8},{12,10},{14,12},{16,14},{18,16},{20... | collective-permute-start | bytes 196616 | tf_op jit(solution)/shard_map/ppermute | solution.py:18
  17.9 1.5 convolution_convert_fusion.4
  19.5 1.3 copy.34
  20.8 1.5 copy.32
  22.3 0.6 convolution_convert_fusion.2
  23.0 1.0 copy-done.24
  23.9 2.2 convolution_add_fusion
  26.2 0.5 convolution_convert_fusion.3
  26.6 0.5 copy-done.26
  27.3 5.4 %all_to_all.10 = bf16[2,1024,512]{2,1,0:T(8,128)(2,1)S(1)} all-to-all(bf16[2,1024,512]{2,1,0:T(8,128)(2,1)S(1)} %broadcast_in_dim.6), channel_id=1, replica_groups=mesh['batch'=2,'space'=64,'hidden'=2] {'hidden'}, dimensions={0} | all-to-all | bytes 4194304 | tf_op jit(solution)/shard_map/all_to_all | solution.py:27
  32.7 1.7 convert_reduce_fusion
  34.3 1.9 copy.33
  36.6 0.3 copy-done.12
  37.0 0.8 convolution_convert_fusion.7
  38.1 0.3 fusion.52
  38.9 0.9 fusion.54
  39.8 0.4 fusion.7
  40.2 0.5 fusion.55
  40.7 0.4 fusion.4
  41.2 1.1 multiply_reduce_fusion
  42.3 0.6 multiply_convert_fusion
  42.9 0.6 copy-done.27
  43.6 0.5 fusion.11
  44.1 0.4 copy-done.22
  44.5 0.7 fusion.53
  45.5 0.4 copy.40
  45.9 0.7 copy-done.7
  46.6 0.3 copy-done.10
  47.0 0.3 copy-done.25
  47.3 1.0 fusion.6
  48.3 0.8 copy.38
  49.2 1.0 constant_dynamic-update-slice_fusion
  50.2 1.4 dynamic-update-slice.1
  51.6 5.2 %dynamic-update-slice.2 = bf16[1312512]{0:T(1024)(128)(2,1)} dynamic-update-slice(bf16[1312512]{0:T(1024)(128)(2,1)} %dynamic-update-slice.1, bf16[131072]{0:T(1024)(128)(2,1)S(1)} %bitcast.92, s32[]{} %constant.47) | dynamic-update-slice | bytes 524292
  56.8 1.4 dynamic-update-slice.3
  58.2 16.8 %dynamic-update-slice.4 = bf16[1312512]{0:T(1024)(128)(2,1)} dynamic-update-slice(bf16[1312512]{0:T(1024)(128)(2,1)} %dynamic-update-slice.3, bf16[524288]{0:T(1024)(128)(2,1)S(1)} %bitcast.84, s32[]{} %constant.49) | dynamic-update-slice | bytes 2097156
  75.1 1.5 dynamic-update-slice.5
  76.6 8.9 %dynamic-update-slice.6 = bf16[1312512]{0:T(1024)(128)(2,1)} dynamic-update-slice(bf16[1312512]{0:T(1024)(128)(2,1)} %dynamic-update-slice.5, bf16[262144]{0:T(1024)(128)(2,1)S(1)} %bitcast.86, s32[]{} %constant.51) | dynamic-update-slice | bytes 1048580
  85.5 1.3 dynamic-update-slice.7
  86.9 1.6 convert_element_type.144
  88.5 1.3 constant_dynamic-slice_fusion
  89.8 0.3 copy.36
  90.1 2.3 fusion.56
  92.6 1.4 fusion.2
  94.0 1.1 fusion.13
  95.3 4.8 %all_to_all.11 = bf16[2,1280,256]{2,1,0:T(8,128)(2,1)S(1)} all-to-all(bf16[2,1280,256]{2,1,0:T(8,128)(2,1)S(1)} %bitcast.83), channel_id=1, replica_groups=mesh['batch'=2,'space'=64,'hidden'=2] {'hidden'}, dimensions={0} | all-to-all | bytes 2621440 | tf_op jit(solution)/shard_map/all_to_all | solution.py:44
  100.5 6.5 %collective-permute-start.3 = (bf16[1,64,256]{2,1,0:T(8,128)(2,1)S(1)}, bf16[1,64,256]{2,1,0:T(8,128)(2,1)S(1)}, u32[]{:S(2)}, u32[]{:S(2)}) collective-permute-start(bf16[1,64,256]{2,1,0:T(8,128)(2,1)S(1)} %get-tuple-element.22), channel_id=1, source_target_pairs={{2,0},{4,2},{6,4},{8,6},{10,8},{12,10},{14,12},{16,14},{18,16},{20... | collective-permute-start | bytes 98312 | tf_op jit(solution)/shard_map/ppermute | solution.py:18
  107.0 0.9 fusion.22
  108.0 1.4 collective-permute-done.2
  109.4 1.9 fusion.17
  111.3 205.7 %all-reduce.2.cloned.1.call-done = bf16[1312512]{0:T(1024)(128)(2,1)} async-done(((bf16[1312512]{0:T(1024)(128)(2,1)}), bf16[1312512]{0:T(1024)(128)(2,1)}) %all-reduce.2.cloned.1.call-update) | async-done | bytes 2625040 | tf_op jit(solution)/shard_map/psum | solution.py:61
  317.0 1.0 slice_convert_fusion.4
  318.0 0.9 reshape.116
  318.9 1.1 slice_convert_fusion.3
  320.0 1.1 reshape.118
  321.2 1.4 slice_convert_fusion.1
  322.6 1.5 reshape.117
  324.1 1.2 slice_convert_fusion.2
  325.3 1.6 reshape.115
  326.9 1.2 slice_convert_fusion.11
  328.1 1.3 slice_convert_fusion.8
  (78 shorter events, 2.4 us)
Async XLA Ops:
  7.2 30.6 %copy-start = (bf16[1024,512]{1,0:T(8,128)(2,1)S(1)}, bf16[1024,512]{1,0:T(8,128)(2,1)}, u32[]{:S(2)}) copy-start(bf16[1024,512]{1,0:T(8,128)(2,1)} %param.26) | copy-start | bytes 3145732
  7.2 12.2 %copy-start.8 = (bf16[1,1024,512]{2,1,0:T(8,128)(2,1)S(1)}, bf16[1,1024,512]{2,1,0:T(8,128)(2,1)}, u32[]{:S(2)}) copy-start(bf16[1,1024,512]{2,1,0:T(8,128)(2,1)} %param.18) | copy-start | bytes 3145732
  7.2 309.8 %all-reduce.2.cloned.1.call-start = ((), (), s32[]{:S(2)}) async-start(), calls=%async_computation.2 | async-start | bytes 5251072 | tf_op jit(solution)/shard_map/psum | solution.py:61
  8.1 3.2 copy-start.17
  9.3 13.0 %collective-permute-start = (bf16[1,64,512]{2,1,0:T(8,128)(2,1)S(1)}, bf16[1,64,512]{2,1,0:T(8,128)(2,1)S(1)}, u32[]{:S(2)}, u32[]{:S(2)}) collective-permute-start(bf16[1,64,512]{2,1,0:T(8,128)(2,1)S(1)} %get-tuple-element.25), channel_id=1, source_target_pairs={{0,2},{2,4},{4,6},{6,8},{8,10},{10,12},{12,14},{14,16},{16,18},{18... | collective-permute-start | bytes 196616 | tf_op jit(solution)/shard_map/ppermute | solution.py:16
  11.3 11.0 %collective-permute-start.1 = (bf16[1,64,512]{2,1,0:T(8,128)(2,1)S(1)}, bf16[1,64,512]{2,1,0:T(8,128)(2,1)S(1)}, u32[]{:S(2)}, u32[]{:S(2)}) collective-permute-start(bf16[1,64,512]{2,1,0:T(8,128)(2,1)S(1)} %get-tuple-element.26), channel_id=1, source_target_pairs={{2,0},{4,2},{6,4},{8,6},{10,8},{12,10},{14,12},{16,14},{18,16},{20... | collective-permute-start | bytes 196616 | tf_op jit(solution)/shard_map/ppermute | solution.py:18
  19.4 3.5 %copy-start.6 = (bf16[1024,512]{0,1:T(8,128)(2,1)}, bf16[1024,512]{0,1:T(8,128)(2,1)S(1)}, u32[]{:S(2)}) copy-start(bf16[1024,512]{0,1:T(8,128)(2,1)S(1)} %convolution_convert_fusion.4) | copy-start | bytes 3145732
  19.4 2.9 copy-start.3
  19.5 2.9 copy-start.14
  20.8 3.1 copy-start.23
  22.3 3.8 %copy-start.9 = (bf16[1,1024,512]{1,2,0:T(8,128)(2,1)}, bf16[1,1024,512]{1,2,0:T(8,128)(2,1)S(1)}, u32[]{:S(2)}) copy-start(bf16[1,1024,512]{1,2,0:T(8,128)(2,1)S(1)} %copy.32) | copy-start | bytes 3145732
  22.9 1.0 copy-start.24
  23.9 2.2 copy-start.21
  26.1 1.0 copy-start.26
  36.3 0.7 copy-start.12
  36.3 0.7 copy-start.13
  36.3 1.5 copy-start.15
  36.6 1.5 copy-start.20
  37.8 0.9 copy-start.11
  37.8 0.9 copy-start.16
  39.8 1.4 copy-start.1
  40.7 1.6 copy-start.4
  42.3 1.2 copy-start.27
  43.5 0.9 copy-start.22
  45.2 3.1 copy-start.5
  45.2 1.4 copy-start.7
  45.2 1.7 copy-start.10
  45.3 2.0 copy-start.25
  49.2 25.9 %copy-start.19 = (bf16[512]{0:T(512)(128)(2,1)S(1)}, bf16[512]{0:T(512)(128)(2,1)}, u32[]{:S(2)}) copy-start(bf16[512]{0:T(512)(128)(2,1)} %get-tuple-element.32) | copy-start | bytes 3076
  75.1 11.8 %copy-start.2 = (bf16[1,1024,512]{1,2,0:T(8,128)(2,1)S(1)}, bf16[1,1024,512]{1,2,0:T(8,128)(2,1)}, u32[]{:S(2)}) copy-start(bf16[1,1024,512]{1,2,0:T(8,128)(2,1)} %copy.34) | copy-start | bytes 3145732
  100.3 9.1 %copy-start.18 = (s32[128]{0:T(128)S(1)}, s32[128]{0:T(128)}, u32[]{:S(2)}) copy-start(s32[128]{0:T(128)} %copy-done.17) | copy-start | bytes 1540
  100.4 9.0 %collective-permute-start.2 = (bf16[1,64,256]{2,1,0:T(8,128)(2,1)S(1)}, bf16[1,64,256]{2,1,0:T(8,128)(2,1)S(1)}, u32[]{:S(2)}, u32[]{:S(2)}) collective-permute-start(bf16[1,64,256]{2,1,0:T(8,128)(2,1)S(1)} %get-tuple-element.21), channel_id=1, source_target_pairs={{0,2},{2,4},{4,6},{6,8},{8,10},{10,12},{12,14},{14,16},{16,18},{18... | collective-permute-start | bytes 98312 | tf_op jit(solution)/shard_map/ppermute | solution.py:16
  100.5 8.9 %collective-permute-start.3 = (bf16[1,64,256]{2,1,0:T(8,128)(2,1)S(1)}, bf16[1,64,256]{2,1,0:T(8,128)(2,1)S(1)}, u32[]{:S(2)}, u32[]{:S(2)}) collective-permute-start(bf16[1,64,256]{2,1,0:T(8,128)(2,1)S(1)} %get-tuple-element.22), channel_id=1, source_target_pairs={{2,0},{4,2},{6,4},{8,6},{10,8},{12,10},{14,12},{16,14},{18,16},{20... | collective-permute-start | bytes 98312 | tf_op jit(solution)/shard_map/ppermute | solution.py:18
Sparse Core Ops, SparseCore 0:
  87.0 229.9 all-reduce.1
where the time goes:
time: 340 us; the launch traced here: 336 us
  waiting for transfers between devices  207 us (61%)
  local copies, waits for them, and re-layouts  56.2 us (17%)
  matrix products  19.6 us (6%)
  starting transfers between devices  15.3 us (4%)
  between operations  14.7 us (4%)
  other arithmetic  13.2 us (4%)
  blocking collectives  10.2 us (3%)
    psum x1, waiting for transfers between devices, in_one(): so_far = lax.psum(jnp.concatenate([a.ravel() for a in arrays]), axis)  206 us
    unnamed x69, local copies, waits for them, and re-layouts  45 us
    ppermute x2, starting transfers between devices, extended(): lax.ppermute(head, axis, [((i + 1) % count, i) for i in range(count)])  13.2 us
    dot_general x8, matrix products, matmul(): return jnp.dot(lefthand, righthand, preferred_element_type=jnp.float32)  7.6 us
    convert_element_type x6, other arithmetic, on_device(): part.astype(jnp.float32)  7.33 us
  transfers between devices with their start and end apart: 5, of which 2 were waited for; matrix products, arithmetic and copies ran while one was open for 5% of the time, Pallas kernels for 0%

commit v1 on v0

--- a/solution.py
+++ b/solution.py
@@ -1,6 +1,8 @@
 import jax
 import jax.numpy as jnp
 from jax import lax
+from jax.experimental import pallas as pl
+from jax.experimental.pallas import tpu as pltpu
 from jax.sharding import PartitionSpec as P
 
 EPS = 1e-05
@@ -110,6 +112,279 @@
 def silu_slope(values):
     logistic = jax.nn.sigmoid(values)
     return logistic * (1.0 + values * (1.0 - logistic))
+
+
+ROWS = 2048
+COLOR = ROWS // 2
+WIDE = COLOR // 4
+NARROW = WIDE // 4
+ZROWS = 2 * NARROW // 8
+NODE_ROWS = 768
+NODE_AT = 1024
+MESH = pl.DeviceIdType.MESH
+
+
+def rows_at(ref, start, count):
+    return ref.at[pl.ds(pl.multiple_of(start, 16), count)]
+
+
+def load_rows(ref, start, count):
+    return ref[pl.ds(pl.multiple_of(start, 16), count), :].astype(jnp.float32)
+
+
+def remote(src, dst, sems, k, device):
+    return pltpu.make_async_remote_copy(
+        src_ref=src,
+        dst_ref=dst,
+        send_sem=sems.at[0, k],
+        recv_sem=sems.at[1, k],
+        device_id=device,
+        device_id_type=MESH,
+    )
+
+
+def scatter_start(src, base, n, d, ahead, behind, held, sems):
+    h = n // 2
+    far, up, down = (base + lax.rem(d + k, 4) * n for k in (2, 1, 3))
+    copies = [
+        remote(rows_at(src, far, h), held.at[0], sems, 0, ahead),
+        remote(rows_at(src, far + h, h), held.at[1], sems, 1, behind),
+        remote(rows_at(src, up + h, h), held.at[2], sems, 2, ahead),
+        remote(rows_at(src, down, h), held.at[3], sems, 3, behind),
+    ]
+    for c in copies:
+        c.start()
+    return copies
+
+
+def scatter_middle(src, base, n, d, ahead, behind, held, made, sems, copies):
+    h = n // 2
+    up, down = (base + lax.rem(d + k, 4) * n for k in (1, 3))
+    copies[0].wait_recv()
+    made[0] = (load_rows(src, up, h) + held[0].astype(jnp.float32)).astype(jnp.bfloat16)
+    c = remote(made.at[0], held.at[4], sems, 4, ahead)
+    c.start()
+    copies.append(c)
+    copies[1].wait_recv()
+    made[1] = (load_rows(src, down + h, h) + held[1].astype(jnp.float32)).astype(jnp.bfloat16)
+    c = remote(made.at[1], held.at[5], sems, 5, behind)
+    c.start()
+    copies.append(c)
+
+
+def scatter_end(src, base, n, d, held, dst, at, copies):
+    h = n // 2
+    own = base + d * n
+    for k in (3, 4):
+        copies[k].wait_recv()
+    dst[pl.ds(at, h), :] = (
+        load_rows(src, own, h) + held[3].astype(jnp.float32) + held[4].astype(jnp.float32)
+    ).astype(jnp.bfloat16)
+    for k in (2, 5):
+        copies[k].wait_recv()
+    dst[pl.ds(at + h, h), :] = (
+        load_rows(src, own + h, h) + held[2].astype(jnp.float32) + held[5].astype(jnp.float32)
+    ).astype(jnp.bfloat16)
+    for c in copies:
+        c.wait_send()
+
+
+def gather_start(out, base, n, d, ahead, behind, sems):
+    h = n // 2
+    own = base + d * n
+    copies = []
+    for k, (at, device) in enumerate(
+        ((own, ahead), (own + h, behind), (own + h, ahead), (own, behind))
+    ):
+        c = remote(rows_at(out, at, h), rows_at(out, at, h), sems, k, device)
+        c.start()
+        copies.append(c)
+    return copies
+
+
+def gather_middle(out, base, n, d, ahead, behind, sems, copies):
+    h = n // 2
+    up, down = (base + lax.rem(d + k, 4) * n for k in (1, 3))
+    for k, (j, at, device) in enumerate(((0, down, ahead), (1, up + h, behind))):
+        copies[j].wait_recv()
+        c = remote(rows_at(out, at, h), rows_at(out, at, h), sems, 4 + k, device)
+        c.start()
+        copies.append(c)
+
+
+def gather_end(copies):
+    for c in copies[2:]:
+        c.wait_recv()
+    for c in copies:
+        c.wait_send()
+
+
+def reduce_kernel(
+    g,
+    out,
+    other,
+    held_wide,
+    made_wide,
+    kept_wide,
+    held_narrow,
+    made_narrow,
+    kept_narrow,
+    held_z,
+    sems_wide,
+    sems_narrow,
+    sems_z,
+    sems_out_z,
+    sems_out_narrow,
+    sems_out_wide,
+    sems_core,
+):
+    batch = lax.axis_index("batch")
+    space = lax.axis_index("space")
+    core = lax.axis_index("hidden")
+    x = space // 16
+    y = (space // 8) % 2 * 2 + batch
+    z = space % 8
+
+    def device(i, j, k):
+        return (j % 2, (i * 2 + j // 2) * 8 + k, core)
+
+    x_up, x_down = (device((x + k) % 4, y, z) for k in (1, 3))
+    y_up, y_down = (device(x, (y + k) % 4, z) for k in (1, 3))
+    z_peers = [device(x, y, (z + k) % 8) for k in range(1, 8)]
+    partner = (batch, space, 1 - core)
+    barrier = pltpu.get_barrier_semaphore()
+    peers = [x_up, x_down, y_up, y_down, *z_peers, partner]
+    for peer in peers:
+        pl.semaphore_signal(barrier, inc=1, device_id=peer, device_id_type=MESH)
+    pl.semaphore_wait(barrier, len(peers))
+
+    along = ((x, x_up, x_down), (y, y_up, y_down))
+    started = []
+    for color in (0, 1):
+        pos, ahead, behind = along[color]
+        started.append(
+            scatter_start(
+                g, color * COLOR, WIDE, pos, ahead, behind, held_wide.at[color], sems_wide.at[color]
+            )
+        )
+    for color in (0, 1):
+        pos, ahead, behind = along[color]
+        scatter_middle(
+            g, color * COLOR, WIDE, pos, ahead, behind, held_wide.at[color],
+            made_wide.at[color], sems_wide.at[color], started[color],
+        )
+    second = []
+    for color in (0, 1):
+        pos, ahead, behind = along[color]
+        scatter_end(
+            g, color * COLOR, WIDE, pos, held_wide.at[color], kept_wide.at[color], 0, started[color]
+        )
+        pos, ahead, behind = along[1 - color]
+        second.append(
+            scatter_start(
+                kept_wide.at[color], 0, NARROW, pos, ahead, behind,
+                held_narrow.at[color], sems_narrow.at[color],
+            )
+        )
+    for color in (0, 1):
+        pos, ahead, behind = along[1 - color]
+        scatter_middle(
+            kept_wide.at[color], 0, NARROW, pos, ahead, behind, held_narrow.at[color],
+            made_narrow.at[color], sems_narrow.at[color], second[color],
+        )
+    for color in (0, 1):
+        pos, ahead, behind = along[1 - color]
+        scatter_end(
+            kept_wide.at[color], 0, NARROW, pos, held_narrow.at[color],
+            kept_narrow, color * NARROW, second[color],
+        )
+    third = []
+    for k in range(1, 8):
+        c = remote(
+            rows_at(kept_narrow, (z + k) % 8 * ZROWS, ZROWS), held_z.at[k - 1], sems_z, k - 1,
+            z_peers[k - 1],
+        )
+        c.start()
+        third.append(c)
+    total = load_rows(kept_narrow, z * ZROWS, ZROWS)
+    for k in range(7):
+        third[k].wait_recv()
+        total = total + held_z[k].astype(jnp.float32)
+    base = (x * WIDE + y * NARROW, COLOR + y * WIDE + x * NARROW)
+    upper = z // 4
+    mine = (1 - upper) * base[0] + upper * base[1] + z % 4 * ZROWS
+    out[pl.ds(pl.multiple_of(mine, 16), ZROWS), :] = total.astype(jnp.bfloat16)
+    for c in third:
+        c.wait_send()
+    third = []
+    for k in range(1, 8):
+        c = remote(rows_at(out, mine, ZROWS), rows_at(out, mine, ZROWS), sems_out_z, k - 1, z_peers[k - 1])
+        c.start()
+        third.append(c)
+    for c in third:
+        c.wait_recv()
+    for c in third:
+        c.wait_send()
+    bases = ((0 + x * WIDE), (COLOR + y * WIDE))
+    copies = []
+    for color in (0, 1):
+        pos, ahead, behind = along[1 - color]
+        copies.append(gather_start(out, bases[color], NARROW, pos, ahead, behind, sems_out_narrow.at[color]))
+    for color in (0, 1):
+        pos, ahead, behind = along[1 - color]
+        gather_middle(out, bases[color], NARROW, pos, ahead, behind, sems_out_narrow.at[color], copies[color])
+    wide = []
+    for color in (0, 1):
+        gather_end(copies[color])
+        pos, ahead, behind = along[color]
+        wide.append(gather_start(out, color * COLOR, WIDE, pos, ahead, behind, sems_out_wide.at[color]))
+    for color in (0, 1):
+        pos, ahead, behind = along[color]
+        gather_middle(out, color * COLOR, WIDE, pos, ahead, behind, sems_out_wide.at[color], wide[color])
+    for color in (1, 0):
+        gather_end(wide[color])
+        if color == 1:
+            c = remote(out.at[pl.ds(NODE_AT, NODE_ROWS)], other, sems_core, 0, partner)
+            c.start()
+    c.wait()
+
+
+def reduce_all(packed):
+    dma = pltpu.SemaphoreType.DMA
+    bf16 = jnp.bfloat16
+    columns = packed.shape[1]
+    vmem = pl.BlockSpec(memory_space=pltpu.VMEM)
+    return pl.pallas_call(
+        reduce_kernel,
+        out_shape=(
+            jax.ShapeDtypeStruct(packed.shape, bf16),
+            jax.ShapeDtypeStruct((NODE_ROWS, columns), bf16),
+        ),
+        in_specs=[vmem],
+        out_specs=(vmem, vmem),
+        scratch_shapes=[
+            pltpu.VMEM((2, 6, WIDE // 2, columns), bf16),
+            pltpu.VMEM((2, 2, WIDE // 2, columns), bf16),
+            pltpu.VMEM((2, WIDE, columns), bf16),
+            pltpu.VMEM((2, 6, NARROW // 2, columns), bf16),
+            pltpu.VMEM((2, 2, NARROW // 2, columns), bf16),
+            pltpu.VMEM((2 * NARROW, columns), bf16),
+            pltpu.VMEM((7, ZROWS, columns), bf16),
+            dma((2, 2, 6)),
+            dma((2, 2, 6)),
+            dma((2, 7)),
+            dma((2, 7)),
+            dma((2, 2, 6)),
+            dma((2, 2, 6)),
+            dma((2, 1)),
+        ],
+        compiler_params=pltpu.CompilerParams(collective_id=1, has_side_effects=True),
+        name="reduce_all",
+    )(packed)
+
+
+def halves_of(part, count, my_part):
+    return lax.dynamic_slice_in_dim(part, my_part * count, count, 0)
 
 
 def on_device(
@@ -204,33 +479,42 @@
     ]
     own_edge_cot = lax.dynamic_slice_in_dim(edge_upstream, my_part * half, half, 1)
     grad_edges = (own_edge_cot + edge_own).astype(jnp.bfloat16)[None]
-    (
-        edge_first_grad,
-        edge_bias_grad,
-        edge_second_grad,
-        edge_gain_grad,
-        node_first_grad,
-        node_bias_grad,
-        node_second_grad,
-        node_gain_grad,
-    ) = tuple(
-        (
-            part.astype(jnp.float32)
-            for part in in_one(
-                (
-                    edge_first_grad.astype(jnp.bfloat16),
-                    edge_bias_grad.astype(jnp.bfloat16),
-                    edge_second_grad.astype(jnp.bfloat16),
-                    edge_gain_grad.astype(jnp.bfloat16),
-                    node_first_grad.astype(jnp.bfloat16),
-                    node_bias_grad.astype(jnp.bfloat16),
-                    node_second_grad.astype(jnp.bfloat16),
-                    node_gain_grad.astype(jnp.bfloat16),
-                ),
-                ("batch", "space"),
-            )
-        )
-    )
+    bf16 = jnp.bfloat16
+    first_rows = edge_first_grad.shape[0] // 2
+    small = jnp.stack(
+        [
+            jnp.concatenate([edge_bias_grad, edge_bias_grad]),
+            edge_gain_grad,
+            node_bias_grad,
+            node_gain_grad,
+        ]
+    )
+    packed = jnp.concatenate(
+        [
+            jnp.concatenate(
+                [edge_first_grad[:first_rows], edge_first_grad[first_rows:]], axis=1
+            ).astype(bf16),
+            edge_second_grad.astype(bf16),
+            halves_of(node_first_grad.astype(bf16), 512, my_part),
+            halves_of(node_second_grad.astype(bf16), 256, my_part),
+            jnp.pad(small, ((0, 252), (0, 0))).astype(bf16),
+        ],
+        axis=0,
+    )
+    summed, other = reduce_all(packed)
+    f32 = jnp.float32
+    edge_first_grad = jnp.concatenate(
+        [summed[:first_rows, :256], summed[:first_rows, 256:]], axis=0
+    ).astype(f32)
+    edge_second_grad = summed[768:1024].astype(f32)
+    own = summed[1024:1792]
+    lower = jnp.where(my_part == 0, own, other)
+    upper = jnp.where(my_part == 0, other, own)
+    node_first_grad = jnp.concatenate([lower[:512], upper[:512]], axis=0).astype(f32)
+    node_second_grad = jnp.concatenate([lower[512:], upper[512:]], axis=0).astype(f32)
+    small = summed[1792:1796].astype(f32)
+    edge_bias_grad = small[0, :256]
+    edge_gain_grad, node_bias_grad, node_gain_grad = small[1], small[2], small[3]
     return (
         grad_nodes,
         grad_edges,

time: 340 us -> 138 us (0.41)
  the two profiles are of different devices: /device:TPU:2 before, /device:TPU:1 now
where the time goes in v1:
time: 138 us; the launch traced here: 137 us
  Pallas kernels  54.1 us (39%)
  local copies, waits for them, and re-layouts  20.3 us (15%)
  starting transfers between devices  18.4 us (13%)
  matrix products  17.9 us (13%)
  other arithmetic  14.7 us (11%)
  blocking collectives  10.6 us (8%)
    pallas_call x1, Pallas kernels, reduce_all(): pl.pallas_call(reduce_kernel, out_shape=(jax.ShapeDtypeStruct(packed.shap...  54.1 us
    ppermute x2, starting transfers between devices, extended(): lax.ppermute(head, axis, [((i + 1) % count, i) for i in range(count)])  15.9 us
    unnamed x60, local copies, waits for them, and re-layouts  11.2 us
    dot_general x8, matrix products, matmul(): return jnp.dot(lefthand, righthand, preferred_element_type=jnp.float32)  7.86 us
    all_to_all x1, blocking collectives, copy_for_each(): lax.all_to_all(jnp.broadcast_to(value[None], (devices, *value.shape)), ax...  5.99 us
    all_to_all x1, blocking collectives, sent_and_summed(): lax.all_to_all(cut_along(value, dim, devices), axis, 0, 0, tiled=True)  4.65 us
    dot_general x3, matrix products, exact_tn(): lax.dot_general(lefthand, righthand, (((0,), (0,)), ((), ())), precision=...  4.39 us
    dot_general x5, matrix products, matmul_tn(): lax.dot_general(lefthand, righthand, (((0,), (0,)), ((), ())), preferred_...  3.17 us
  transfers between devices with their start and end apart: 4, of which 0 were waited for; matrix products, arithmetic and copies ran while one was open for 10% of the time, Pallas kernels for 0%

profile of v1, /device:TPU:1, one launch (start us, length us, event | category | flops | bytes accessed | tf_op | source)
XLA Modules:
  0.0 137.4 jit_solution(10553450535949245789)
XLA Ops:
  0.7 0.9 eq.28
  1.5 1.1 convolution_convert_fusion.6
  2.7 0.7 slice_bitcast_fusion.1
  3.3 2.5 %collective-permute-start = (bf16[1,64,512]{2,1,0:T(8,128)(2,1)}, bf16[1,64,512]{2,1,0:T(8,128)(2,1)}, u32[]{:S(2)}, u32[]{:S(2)}) collective-permute-start(bf16[1,64,512]{2,1,0:T(8,128)(2,1)} %get-tuple-element.32), channel_id=1, source_target_pairs={{0,2},{2,4},{4,6},{6,8},{8,10},{10,12},{12,14},{14,16},{16,18},{18... | collective-permute-start | bytes 196616 | tf_op jit(solution)/shard_map/ppermute | solution.py:18
  5.8 8.8 %collective-permute-start.1 = (bf16[1,64,512]{2,1,0:T(8,128)(2,1)}, bf16[1,64,512]{2,1,0:T(8,128)(2,1)}, u32[]{:S(2)}, u32[]{:S(2)}) collective-permute-start(bf16[1,64,512]{2,1,0:T(8,128)(2,1)} %get-tuple-element.33), channel_id=1, source_target_pairs={{2,0},{4,2},{6,4},{8,6},{10,8},{12,10},{14,12},{16,14},{18,16},{20... | collective-permute-start | bytes 196616 | tf_op jit(solution)/shard_map/ppermute | solution.py:20
  14.5 1.5 %copy.36 = bf16[1,1024,512]{1,2,0:T(8,128)(2,1)S(1)} copy(bf16[1,1024,512]{2,1,0:T(8,128)(2,1)} %param.18) | data formatting | bytes 2097152 | tf_op args[3]
  16.1 0.6 convolution_convert_fusion.3
  16.6 1.7 %convert_element_type.120 = f32[1,1024,512]{1,2,0:T(8,128)} convert(bf16[1,1024,512]{1,2,0:T(8,128)(2,1)S(1)} %copy.36) | non-fusion elementwise | flops 524288 | bytes 3145728 | tf_op jit(solution)/shard_map/convert_element_type | solution.py:446
  18.3 1.3 constant_dynamic-slice_fusion
  19.6 0.9 convert_element_type.107
  20.6 2.3 %copy.34 = bf16[1,1024,512]{1,2,0:T(8,128)(2,1)} copy(bf16[1,1024,512]{2,1,0:T(8,128)(2,1)} %param.16) | data formatting | bytes 2097152 | tf_op args[1]
  22.8 1.3 copy.38
  24.2 1.5 %convolution_convert_fusion.1 = bf16[1024,512]{0,1:T(8,128)(2,1)S(1)} fusion(s32[1024]{0:T(1024)S(1)} %copy-done.17, bf16[64,512]{1,0:T(8,128)(2,1)} %bitcast.6, bf16[64,512]{1,0:T(8,128)(2,1)} %bitcast.4, bf16[128,512]{1,0:T(8,128)(2,1)S(1)} %bitcast.76), kind=kOutput, calls=%fused_computation.18 | convolution fusion | flops 270008320 | bytes 1314816 | tf_op jit(solution)/shard_map/dot_general | solution.py:72
  25.7 1.0 copy-done.24
  26.6 2.5 %convolution_add_fusion = f32[1024,256]{1,0:T(8,128)S(1)} fusion(bf16[1536,256]{1,0:T(8,128)(2,1)} %param.22, bf16[1024,512]{0,1:T(8,128)(2,1)S(1)} %convolution_convert_fusion.3, bf16[1024,512]{0,1:T(8,128)(2,1)S(1)} %convolution_convert_fusion.1, bf16[1024,512]{0,1:T(8,128)(2,1)} %bitcast.79, f32[256]{0:T(256)S(1)} %copy-done.23), kind=kOutput, calls=%fused_computation.24 | convolution fusion | flops 815005696 | bytes 4981760 | tf_op jit(solution)/shard_map/dot_general | solution.py:72
  29.2 0.5 convolution_convert_fusion.2
  29.6 0.5 copy-done.26
  30.1 0.1 broadcast_in_dim.6
  30.3 6.0 %all_to_all.10 = bf16[2,1024,512]{2,1,0:T(8,128)(2,1)S(1)} all-to-all(bf16[2,1024,512]{2,1,0:T(8,128)(2,1)S(1)} %broadcast_in_dim.6), channel_id=1, replica_groups=mesh['batch'=2,'space'=64,'hidden'=2] {'hidden'}, dimensions={0} | all-to-all | bytes 4194304 | tf_op jit(solution)/shard_map/all_to_all | solution.py:29
  36.2 1.7 %convert_reduce_fusion = (f32[1024]{0:T(1024)S(1)}, f32[1024,512]{1,0:T(8,128)}) fusion(bf16[2,1024,512]{2,1,0:T(8,128)(2,1)S(1)} %all_to_all.10), kind=kLoop, calls=%fused_computation | loop fusion | flops 2620416 | bytes 4198400 | tf_op jit(solution)/shard_map/reduce_sum | solution.py:98
  37.9 2.1 %copy.35 = f32[1024,512]{0,1:T(8,128)S(1)} copy(f32[1024,512]{1,0:T(8,128)} %get-tuple-element.18) | data formatting | bytes 4194304 | tf_op jit(solution)/shard_map/reduce_sum | solution.py:35
  40.0 0.3 multiply_reduce_fusion.2
  40.3 0.3 copy-done.16
  40.7 0.8 convolution_convert_fusion.5
  41.5 0.3 convolution_add_fusion.1
  41.9 0.3 fusion.64
  42.2 0.2 multiply_reduce_fusion.5
  42.4 0.2 fusion.39
  42.7 0.3 fusion.65
  43.0 0.4 fusion.59
  43.4 0.5 fusion.67
  43.9 0.4 fusion.45
  44.4 1.1 multiply_reduce_fusion
  45.6 0.6 multiply_convert_fusion
  46.1 0.4 copy-done.22
  46.5 0.4 copy-done.27
  46.9 0.7 fusion.66
  47.6 0.5 copy-done.10
  48.1 0.3 copy-done.11
  48.4 0.5 copy-done.25
  48.9 1.0 convolution_convert_fusion
  50.1 0.5 fusion.5
  50.7 1.3 copy-done.4
  52.0 54.1 %reduce_all.1 = (bf16[2048,512]{1,0:T(8,128)(2,1)}, bf16[768,512]{1,0:T(8,128)(2,1)}) custom-call(bf16[2048,512]{1,0:T(8,128)(2,1)} %copy-done.4), custom_call_target="tpu_custom_call" | custom-call | tf_op jit(solution)/shard_map/reduce_all/pallas_call | solution.py:357
  106.2 0.8 slice_convert_fusion.5
  106.9 1.8 %slice_convert_fusion.3 = f32[256,512]{1,0:T(8,128)} fusion(bf16[2048,512]{1,0:T(8,128)(2,1)} %get-tuple-element.12), kind=kLoop, calls=%fused_computation.81 | loop fusion | flops 131072 | bytes 786432 | tf_op jit(solution)/shard_map/convert_element_type | solution.py:509
  108.7 1.2 fusion.61
  109.9 1.2 broadcast_select_fusion.1
  111.3 0.9 copy-done.8
  112.2 0.3 copy-done.13
  112.5 1.0 fusion.68
  113.5 1.4 %fusion.2 = f32[256,512]{1,0:T(8,128)S(1)} fusion(f32[1024,1536]{1,0:T(8,128)S(1)} %fusion.68, s32[1024]{0:T(1024)S(1)} %copy-done.17), kind=kOutput, calls=%fused_computation.7 | convolution fusion | flops 1610874880 | bytes 2625536 | tf_op jit(solution)/shard_map/dot_general | solution.py:88
  114.9 1.1 fusion.10
  116.2 0.6 fusion.63
  117.0 4.7 %all_to_all.11 = bf16[2,1280,256]{2,1,0:T(8,128)(2,1)S(1)} all-to-all(bf16[2,1280,256]{2,1,0:T(8,128)(2,1)S(1)} %bitcast.75), channel_id=1, replica_groups=mesh['batch'=2,'space'=64,'hidden'=2] {'hidden'}, dimensions={0} | all-to-all | bytes 2621440 | tf_op jit(solution)/shard_map/all_to_all | solution.py:46
  121.6 0.2 convert_reduce_fusion.2
  121.9 0.9 copy-done.3
  122.8 0.9 fusion.19
  123.7 7.2 %collective-permute-start.3 = (bf16[1,64,256]{2,1,0:T(8,128)(2,1)S(1)}, bf16[1,64,256]{2,1,0:T(8,128)(2,1)S(1)}, u32[]{:S(2)}, u32[]{:S(2)}) collective-permute-start(bf16[1,64,256]{2,1,0:T(8,128)(2,1)S(1)} %get-tuple-element.29), channel_id=1, source_target_pairs={{2,0},{4,2},{6,4},{8,6},{10,8},{12,10},{14,12},{16,14},{18,16},{20... | collective-permute-start | bytes 98312 | tf_op jit(solution)/shard_map/ppermute | solution.py:20
  130.9 1.3 maximum_convert_fusion.1
  132.2 1.6 %maximum_convert_fusion = f32[1024,512]{1,0:T(8,128)} fusion(bf16[512,512]{1,0:T(8,128)(2,1)S(1)} %slice.148, bf16[512,512]{1,0:T(8,128)(2,1)S(1)} %slice.147), kind=kLoop, calls=%fused_computation.41 | loop fusion | flops 2097152 | bytes 3145728 | tf_op jit(solution)/shard_map/convert_element_type | solution.py:513
  133.8 1.1 maximum_convert_fusion.2
  134.9 0.6 slice.145
  135.5 1.9 %fusion.14 = bf16[1,128,256]{2,1,0:T(8,128)(2,1)} fusion(f32[1280,256]{1,0:T(8,128)S(1)} %convert_reduce_fusion.2, f32[64,256]{1,0:T(8,128)S(1)} %get-tuple-element.31, f32[64,256]{1,0:T(8,128)S(1)} %get-tuple-element.30, f32[128,1024]{1,0:T(8,128)} %copy-done.6, s32[]{:T(128)S(6)} %select_n.24, f32[1,128,512]{2,1,0:T(8,128)S(1)} %convert_element_type.107, ...), kind=kOutput, calls=%fused_computation.37 | convolution fusion | flops 50511872 | bytes 590344 | tf_op jit(solution)/shard_map/dot_general | solution.py:88
  (77 shorter events, 0.9 us)
Async XLA Ops:
  0.6 40.9 %copy-start = (bf16[1024,512]{1,0:T(8,128)(2,1)S(1)}, bf16[1024,512]{1,0:T(8,128)(2,1)}, u32[]{:S(2)}) copy-start(bf16[1024,512]{1,0:T(8,128)(2,1)} %param.26) | copy-start | bytes 3145732
  0.7 15.4 %copy-start.5 = (bf16[1,128,512]{2,1,0:T(8,128)(2,1)S(1)}, bf16[1,128,512]{2,1,0:T(8,128)(2,1)}, u32[]{:S(2)}) copy-start(bf16[1,128,512]{2,1,0:T(8,128)(2,1)} %param.15) | copy-start | bytes 393220
  0.7 15.4 %copy-start.15 = (s32[1024]{0:T(1024)S(1)}, s32[1024]{0:T(1024)}, u32[]{:S(2)}) copy-start(s32[1024]{0:T(1024)} %param.20) | copy-start | bytes 12292
  3.3 20.8 %collective-permute-start = (bf16[1,64,512]{2,1,0:T(8,128)(2,1)}, bf16[1,64,512]{2,1,0:T(8,128)(2,1)}, u32[]{:S(2)}, u32[]{:S(2)}) collective-permute-start(bf16[1,64,512]{2,1,0:T(8,128)(2,1)} %get-tuple-element.32), channel_id=1, source_target_pairs={{0,2},{2,4},{4,6},{6,8},{8,10},{10,12},{12,14},{14,16},{16,18},{18... | collective-permute-start | bytes 196616 | tf_op jit(solution)/shard_map/ppermute | solution.py:18
  5.8 18.4 %collective-permute-start.1 = (bf16[1,64,512]{2,1,0:T(8,128)(2,1)}, bf16[1,64,512]{2,1,0:T(8,128)(2,1)}, u32[]{:S(2)}, u32[]{:S(2)}) collective-permute-start(bf16[1,64,512]{2,1,0:T(8,128)(2,1)} %get-tuple-element.33), channel_id=1, source_target_pairs={{2,0},{4,2},{6,4},{8,6},{10,8},{12,10},{14,12},{16,14},{18,16},{20... | collective-permute-start | bytes 196616 | tf_op jit(solution)/shard_map/ppermute | solution.py:20
  16.1 2.2 %copy-start.1 = (bf16[1,1024,512]{1,2,0:T(8,128)(2,1)}, bf16[1,1024,512]{1,2,0:T(8,128)(2,1)S(1)}, u32[]{:S(2)}) copy-start(bf16[1,1024,512]{1,2,0:T(8,128)(2,1)S(1)} %copy.36) | copy-start | bytes 3145732
  16.6 9.0 %copy-start.9 = (bf16[1024,512]{0,1:T(8,128)(2,1)}, bf16[1024,512]{0,1:T(8,128)(2,1)S(1)}, u32[]{:S(2)}) copy-start(bf16[1024,512]{0,1:T(8,128)(2,1)S(1)} %convolution_convert_fusion.3) | copy-start | bytes 3145732
  20.5 3.6 %copy-start.17 = (s32[1024]{0:T(1024)S(1)}, s32[1024]{0:T(1024)}, u32[]{:S(2)}) copy-start(s32[1024]{0:T(1024)} %param.19) | copy-start | bytes 12292
  22.8 3.8 %copy-start.23 = (f32[256]{0:T(256)S(1)}, f32[256]{0:T(256)}, u32[]{:S(2)}) copy-start(f32[256]{0:T(256)} %param.23) | copy-start | bytes 3076
  25.6 1.0 copy-start.24
  26.6 2.5 %copy-start.21 = (bf16[256,512]{1,0:T(8,128)(2,1)S(1)}, bf16[256,512]{1,0:T(8,128)(2,1)}, u32[]{:S(2)}) copy-start(bf16[256,512]{1,0:T(8,128)(2,1)} %param.24) | copy-start | bytes 786436
  29.1 1.0 copy-start.26
  40.0 0.7 copy-start.16
  40.0 1.5 %copy-start.18 = (f32[512]{0:T(512)S(1)}, f32[512]{0:T(512)}, u32[]{:S(2)}) copy-start(f32[512]{0:T(512)} %param.27) | copy-start | bytes 6148
  40.3 1.5 %copy-start.20 = (bf16[512,512]{1,0:T(8,128)(2,1)S(1)}, bf16[512,512]{1,0:T(8,128)(2,1)}, u32[]{:S(2)}) copy-start(bf16[512,512]{1,0:T(8,128)(2,1)} %param.28) | copy-start | bytes 1572868
  41.5 0.9 copy-start.14
  41.5 0.9 copy-start.19
  43.0 1.4 %copy-start.2 = (bf16[1,1024,512]{1,2,0:T(8,128)(2,1)S(1)}, bf16[1,1024,512]{1,2,0:T(8,128)(2,1)}, u32[]{:S(2)}) copy-start(bf16[1,1024,512]{1,2,0:T(8,128)(2,1)} %copy-done.1) | copy-start | bytes 3145732
  43.9 1.6 %copy-start.6 = (f32[128,1024]{1,0:T(8,128)}, f32[128,1024]{1,0:T(8,128)S(1)}, u32[]{:S(2)}) copy-start(f32[128,1024]{1,0:T(8,128)S(1)} %fusion.67) | copy-start | bytes 1572868
  45.5 1.0 copy-start.22
  45.6 1.3 copy-start.27
  46.9 1.2 copy-start.10
  46.9 1.5 %copy-start.11 = (bf16[1,1024,512]{1,2,0:T(8,128)(2,1)S(1)}, bf16[1,1024,512]{1,2,0:T(8,128)(2,1)}, u32[]{:S(2)}) copy-start(bf16[1,1024,512]{1,2,0:T(8,128)(2,1)} %copy.34) | copy-start | bytes 3145732
  46.9 2.0 %copy-start.25 = (bf16[1024,512]{0,1:T(8,128)(2,1)S(1)}, bf16[1024,512]{0,1:T(8,128)(2,1)}, u32[]{:S(2)}) copy-start(bf16[1024,512]{0,1:T(8,128)(2,1)} %copy-done.24) | copy-start | bytes 3145732
  47.6 2.3 %copy-start.7 = (bf16[1024,256]{1,0:T(8,128)(2,1)}, bf16[1024,256]{1,0:T(8,128)(2,1)S(1)}, u32[]{:S(2)}) copy-start(bf16[1024,256]{1,0:T(8,128)(2,1)S(1)} %get-tuple-element.43) | copy-start | bytes 1572868
  50.7 1.3 copy-start.4
  106.2 3.8 %copy-start.12 = (bf16[768,512]{1,0:T(8,128)(2,1)S(1)}, bf16[768,512]{1,0:T(8,128)(2,1)}, u32[]{:S(2)}) copy-start(bf16[768,512]{1,0:T(8,128)(2,1)} %get-tuple-element.13) | copy-start | bytes 2359300
  111.2 1.0 copy-start.8
  111.2 1.3 copy-start.13
  121.6 1.2 copy-start.3
  123.7 11.7 %collective-permute-start.2 = (bf16[1,64,256]{2,1,0:T(8,128)(2,1)S(1)}, bf16[1,64,256]{2,1,0:T(8,128)(2,1)S(1)}, u32[]{:S(2)}, u32[]{:S(2)}) collective-permute-start(bf16[1,64,256]{2,1,0:T(8,128)(2,1)S(1)} %get-tuple-element.28), channel_id=1, source_target_pairs={{0,2},{2,4},{4,6},{6,8},{8,10},{10,12},{12,14},{14,16},{16,18},{18... | collective-permute-start | bytes 98312 | tf_op jit(solution)/shard_map/ppermute | solution.py:18
  123.7 11.7 %collective-permute-start.3 = (bf16[1,64,256]{2,1,0:T(8,128)(2,1)S(1)}, bf16[1,64,256]{2,1,0:T(8,128)(2,1)S(1)}, u32[]{:S(2)}, u32[]{:S(2)}) collective-permute-start(bf16[1,64,256]{2,1,0:T(8,128)(2,1)S(1)} %get-tuple-element.29), channel_id=1, source_target_pairs={{2,0},{4,2},{6,4},{8,6},{10,8},{12,10},{14,12},{16,14},{18,16},{20... | collective-permute-start | bytes 98312 | tf_op jit(solution)/shard_map/ppermute | solution.py:20

commit v2 on v1

v2 whole, which is shorter than its diff:
```python
import jax
import jax.numpy as jnp
from jax import lax
from jax.experimental import pallas as pl
from jax.experimental.pallas import tpu as pltpu
from jax.sharding import PartitionSpec as P

EPS = 1e-05


def hot_columns(indices, rows):
    wanted = lax.broadcasted_iota(jnp.int32, (rows, indices.shape[1]), 0)
    return jnp.where(wanted == indices, 1.0, 0.0).astype(jnp.bfloat16)


def nn(lefthand, righthand):
    return jnp.dot(lefthand, righthand, preferred_element_type=jnp.float32)


def tn(lefthand, righthand):
    return lax.dot_general(
        lefthand, righthand, (((0,), (0,)), ((), ())), preferred_element_type=jnp.float32
    )


def nt(lefthand, righthand):
    return lax.dot_general(
        lefthand, righthand, (((1,), (1,)), ((), ())), preferred_element_type=jnp.float32
    )


def normalize(values):
    centre = values - jnp.mean(values, axis=-1, keepdims=True)
    scaled = lax.rsqrt(jnp.mean(centre * centre, axis=-1, keepdims=True) + EPS)
    return (centre * scaled, scaled)


def norm_back(pulled, normed, scaled):
    return scaled * (
        pulled
        - jnp.mean(pulled, axis=-1, keepdims=True)
        - normed * jnp.mean(pulled * normed, axis=-1, keepdims=True)
    )


def silu(values):
    return values / (1.0 + jnp.exp(-values))


def silu_slope(values):
    logistic = 1.0 / (1.0 + jnp.exp(-values))
    return logistic * (1.0 + values * (1.0 - logistic))


ROWS = 2048
COLOR = ROWS // 2
WIDE = COLOR // 4
NARROW = WIDE // 4
ZROWS = 2 * NARROW // 8
NODE_ROWS = 784
NODE_AT = 1024
MESH = pl.DeviceIdType.MESH


def rows_at(ref, start, count):
    return ref.at[pl.ds(pl.multiple_of(start, 16), count)]


def load_rows(ref, start, count):
    return ref[pl.ds(pl.multiple_of(start, 16), count), :].astype(jnp.float32)


def remote(src, dst, sems, k, device):
    return pltpu.make_async_remote_copy(
        src_ref=src,
        dst_ref=dst,
        send_sem=sems.at[0, k],
        recv_sem=sems.at[1, k],
        device_id=device,
        device_id_type=MESH,
    )


def scatter_start(src, base, n, d, ahead, behind, held, sems):
    h = n // 2
    far, up, down = (base + lax.rem(d + k, 4) * n for k in (2, 1, 3))
    copies = [
        remote(rows_at(src, far, h), held.at[0], sems, 0, ahead),
        remote(rows_at(src, far + h, h), held.at[1], sems, 1, behind),
        remote(rows_at(src, up + h, h), held.at[2], sems, 2, ahead),
        remote(rows_at(src, down, h), held.at[3], sems, 3, behind),
    ]
    for c in copies:
        c.start()
    return copies


def scatter_middle(src, base, n, d, ahead, behind, held, made, sems, copies):
    h = n // 2
    up, down = (base + lax.rem(d + k, 4) * n for k in (1, 3))
    copies[0].wait_recv()
    made[0] = (load_rows(src, up, h) + held[0].astype(jnp.float32)).astype(jnp.bfloat16)
    c = remote(made.at[0], held.at[4], sems, 4, ahead)
    c.start()
    copies.append(c)
    copies[1].wait_recv()
    made[1] = (load_rows(src, down + h, h) + held[1].astype(jnp.float32)).astype(jnp.bfloat16)
    c = remote(made.at[1], held.at[5], sems, 5, behind)
    c.start()
    copies.append(c)


def scatter_end(src, base, n, d, held, dst, at, copies):
    h = n // 2
    own = base + d * n
    for k in (3, 4):
        copies[k].wait_recv()
    dst[pl.ds(at, h), :] = (
        load_rows(src, own, h) + held[3].astype(jnp.float32) + held[4].astype(jnp.float32)
    ).astype(jnp.bfloat16)
    for k in (2, 5):
        copies[k].wait_recv()
    dst[pl.ds(at + h, h), :] = (
        load_rows(src, own + h, h) + held[2].astype(jnp.float32) + held[5].astype(jnp.float32)
    ).astype(jnp.bfloat16)
    for c in copies:
        c.wait_send()


def gather_start(out, base, n, d, ahead, behind, sems):
    h = n // 2
    own = base + d * n
    copies = []
    for k, (at, device) in enumerate(
        ((own, ahead), (own + h, behind), (own + h, ahead), (own, behind))
    ):
        c = remote(rows_at(out, at, h), rows_at(out, at, h), sems, k, device)
        c.start()
        copies.append(c)
    return copies


def gather_middle(out, base, n, d, ahead, behind, sems, copies):
    h = n // 2
    up, down = (base + lax.rem(d + k, 4) * n for k in (1, 3))
    for k, (j, at, device) in enumerate(((0, down, ahead), (1, up + h, behind))):
        copies[j].wait_recv()
        c = remote(rows_at(out, at, h), rows_at(out, at, h), sems, 4 + k, device)
        c.start()
        copies.append(c)


def gather_end(copies):
    for c in copies[2:]:
        c.wait_recv()
    for c in copies:
        c.wait_send()


EDGES = 1024
NODES = 128
HALO = 64
WIDTH = 512
HALF = 256
TILE = 256
TILES = EDGES // TILE


def places():
    batch = lax.axis_index("batch")
    space = lax.axis_index("space")
    core = lax.axis_index("hidden")
    return (
        core,
        (batch, space, 1 - core),
        (batch, (space + 63) % 64, core),
        (batch, (space + 1) % 64, core),
    )


def layer_kernel(
    nodes,
    listed,
    senders,
    receivers,
    first,
    second,
    edge_bias,
    edge_gain,
    node_bias,
    node_gain,
    edges_far,
    cot_far,
    node_cot_far,
    node_first_far,
    node_second_far,
    g,
    edge_mine,
    edge_send,
    table_mine,
    table_send,
    edges,
    cot,
    node_cot,
    node_first,
    node_second,
    other_first,
    other_second,
    other_bias,
    outgoing,
    table,
    hot,
    pre,
    lifted,
    act,
    normed,
    scale,
    agg,
    node_input,
    node_act,
    agg_grad,
    dz,
    dh,
    sums,
    local_sems,
    sems,
):
    bf16, f32 = jnp.bfloat16, jnp.float32
    core, partner, before, after = places()
    barrier = pltpu.get_barrier_semaphore()
    for peer in (partner, before, after):
        pl.semaphore_signal(barrier, inc=1, device_id=peer, device_id_type=MESH)
    loads = [
        pltpu.make_async_copy(src, dst, local_sems.at[k])
        for k, (src, dst) in enumerate(
            (
                (edges_far, edges),
                (node_first_far, node_first),
                (node_second_far, node_second),
                (node_cot_far, node_cot),
                (cot_far, cot),
            )
        )
    ]
    for c in loads:
        c.start()
    outgoing[...] = tn(hot_columns(listed[...], NODES), nodes[...]).astype(bf16)
    table[0:NODES] = nodes[...]
    pl.semaphore_wait(barrier, 3)
    sent = [
        remote(first, other_first, sems, 0, partner),
        remote(edge_bias, other_bias, sems, 1, partner),
        remote(second, other_second, sems, 2, partner),
        remote(outgoing.at[pl.ds(0, HALO)], table.at[pl.ds(NODES + HALO, HALO)], sems, 3, before),
        remote(outgoing.at[pl.ds(HALO, HALO)], table.at[pl.ds(NODES, HALO)], sems, 4, after),
    ]
    for c in (sent[3], sent[4], sent[0], sent[1], sent[2]):
        c.start()
    for t in range(TILES):
        hot[t, 0 : 2 * NODES] = hot_columns(senders[:, t * TILE : (t + 1) * TILE], 2 * NODES)
        hot[t, 2 * NODES :] = hot_columns(receivers[:, t * TILE : (t + 1) * TILE], NODES)

    def lift(weights, columns):
        for t in range(TILES):
            rows = pl.ds(t * TILE, TILE)
            pre[rows, columns] = nn(edges[rows, :], weights[0:WIDTH])
        lifted[0:NODES, columns] = nn(nodes[...], weights[WIDTH : 2 * WIDTH]).astype(bf16)
        lifted[2 * NODES :, columns] = nn(nodes[...], weights[2 * WIDTH :]).astype(bf16)

    own_columns, other_columns = pl.ds(0, HALF), pl.ds(HALF, HALF)
    loads[0].wait()
    lift(first, own_columns)
    sent[0].wait_recv()
    lift(other_first, other_columns)
    sent[3].wait_recv()
    sent[4].wait_recv()
    for weights, columns in ((first, own_columns), (other_first, other_columns)):
        lifted[NODES : 2 * NODES, columns] = nn(
            table[NODES:], weights[WIDTH : 2 * WIDTH]
        ).astype(bf16)
    sent[1].wait_recv()
    sent[2].wait_recv()
    agg[...] = jnp.zeros_like(agg)

    def forward(t, _):
        rows = pl.ds(pl.multiple_of(t * TILE, TILE), TILE)
        chosen = hot[t]
        own = pre[rows, own_columns] + tn(chosen, lifted[:, own_columns]) + edge_bias[...]
        pre[rows, own_columns] = own
        own_act = silu(own).astype(bf16)
        act[rows, :] = own_act
        theirs = pre[rows, other_columns] + tn(chosen, lifted[:, other_columns]) + other_bias[...]
        out = nn(own_act, second[...]) + nn(silu(theirs).astype(bf16), other_second[...])
        values, scaled = normalize(out)
        normed[rows, :] = values
        scale[rows, :] = scaled
        agg[...] += nn(chosen[2 * NODES :], (edge_gain[...] * values).astype(bf16))
        return 0

    lax.fori_loop(0, TILES, forward, 0)
    node_input[0] = nodes[...]
    node_input[1] = agg[...].astype(bf16)
    for c in loads[1:4]:
        c.wait()
    node_pre = (
        nn(nodes[...], node_first[0:WIDTH]) + nn(node_input[1], node_first[WIDTH:]) + node_bias[...]
    )
    node_act[...] = silu(node_pre).astype(bf16)
    node_normed, node_scale = normalize(nn(node_act[...], node_second[...]))
    upstream = node_cot[...].astype(f32)
    sums[2:3] = jnp.sum(upstream * node_normed, axis=0, keepdims=True)
    node_dz = norm_back(upstream * node_gain[...], node_normed, node_scale).astype(bf16)
    node_dh = (nt(node_dz, node_second[...]) * silu_slope(node_pre)).astype(bf16)
    agg_grad[...] = nt(node_dh, node_first[WIDTH:]).astype(bf16)
    sums[3:4] = jnp.sum(node_dh.astype(f32), axis=0, keepdims=True)
    half_at = pl.multiple_of(core * HALF, HALF)
    other_at = pl.multiple_of((1 - core) * HALF, HALF)
    table_mine[0:NODES] = node_cot[:, pl.ds(half_at, HALF)].astype(f32) + nt(
        node_dh, node_first[pl.ds(half_at, HALF), :]
    )
    g[1024:1536] = tn(node_input[core], node_dh).astype(bf16)
    g[1536:1792] = tn(node_act[:, pl.ds(half_at, HALF)], node_dz).astype(bf16)
    loads[4].wait()
    sums[0:2] = jnp.zeros((2, WIDTH), f32)

    def backward(t, _):
        rows = pl.ds(pl.multiple_of(t * TILE, TILE), TILE)
        pulled = cot[rows, :].astype(f32) + tn(hot[t, 2 * NODES :], agg_grad[...])
        values = normed[rows, :]
        sums[0:1] += jnp.sum(pulled * values, axis=0, keepdims=True)
        tile_dz = norm_back(pulled * edge_gain[...], values, scale[rows, :]).astype(bf16)
        dz[rows, :] = tile_dz
        tile_dh = (nt(tile_dz, second[...]) * silu_slope(pre[rows, own_columns])).astype(bf16)
        dh[rows, :] = tile_dh
        sums[1:2, own_columns] += jnp.sum(tile_dh.astype(f32), axis=0, keepdims=True)
        edge_mine[rows, :] = cot[rows, pl.ds(half_at, HALF)].astype(f32) + nt(
            tile_dh, first[pl.ds(half_at, HALF), :]
        )
        edge_send[rows, :] = nt(tile_dh, first[pl.ds(other_at, HALF), :]).astype(bf16)
        return 0

    lax.fori_loop(0, TILES, backward, 0)
    gathered = sum(nn(hot[t], dh[t * TILE : (t + 1) * TILE]) for t in range(TILES)).astype(bf16)
    from_sender, from_receiver = gathered[0 : 2 * NODES], gathered[2 * NODES :]
    for target, at in ((table_mine, half_at), (table_send, other_at)):
        table_part = nt(from_sender, first[pl.ds(WIDTH + at, HALF), :])
        top = table_part[0:NODES] + nt(from_receiver, first[pl.ds(2 * WIDTH + at, HALF), :])
        if target is table_mine:
            target[0:NODES] += top
        else:
            target[0:NODES] = top.astype(bf16)
        target[NODES:] = table_part[NODES:].astype(target.dtype)
    g[0:512, own_columns] = tn(edges[...], dh[...]).astype(bf16)
    sender_grad = tn(table[...], from_sender).astype(bf16)
    g[512:768, own_columns] = sender_grad[0:256]
    g[0:256, other_columns] = sender_grad[256:512]
    g[256:768, other_columns] = tn(nodes[...], from_receiver).astype(bf16)
    g[768:1024] = tn(act[...], dz[...]).astype(bf16)
    mine = sums[:, pl.ds(half_at, HALF)]
    g[1792:2048] = jnp.zeros((256, WIDTH), bf16)
    row = lax.broadcasted_iota(jnp.int32, (16, HALF), 0)
    g[1792:1808, own_columns] = jnp.where(
        row == 0, sums[1:2, own_columns], jnp.where(row == 1, mine[3:4], 0.0)
    ).astype(bf16)
    g[1792:1808, other_columns] = jnp.where(
        row == 0, mine[0:1], jnp.where(row == 1, mine[2:3], 0.0)
    ).astype(bf16)
    for c in sent:
        c.wait_send()


def layer_call(*operands):
    bf16, f32 = jnp.bfloat16, jnp.float32
    dma = pltpu.SemaphoreType.DMA
    vmem = pl.BlockSpec(memory_space=pltpu.VMEM)
    far = pl.BlockSpec(memory_space=pl.ANY)
    return pl.pallas_call(
        layer_kernel,
        out_shape=(
            jax.ShapeDtypeStruct((ROWS, WIDTH), bf16),
            jax.ShapeDtypeStruct((EDGES, HALF), f32),
            jax.ShapeDtypeStruct((EDGES, HALF), bf16),
            jax.ShapeDtypeStruct((2 * NODES, HALF), f32),
            jax.ShapeDtypeStruct((2 * NODES, HALF), bf16),
        ),
        in_specs=[vmem] * 10 + [far] * 5,
        out_specs=(vmem,) * 5,
        scratch_shapes=[
            pltpu.VMEM((EDGES, WIDTH), bf16),
            pltpu.VMEM((EDGES, WIDTH), bf16),
            pltpu.VMEM((NODES, WIDTH), bf16),
            pltpu.VMEM((2 * WIDTH, WIDTH), bf16),
            pltpu.VMEM((WIDTH, WIDTH), bf16),
            pltpu.VMEM((3 * WIDTH, HALF), bf16),
            pltpu.VMEM((HALF, WIDTH), bf16),
            pltpu.VMEM((1, HALF), f32),
            pltpu.VMEM((NODES, WIDTH), bf16),
            pltpu.VMEM((2 * NODES, WIDTH), bf16),
            pltpu.VMEM((TILES, 3 * NODES, TILE), bf16),
            pltpu.VMEM((EDGES, WIDTH), f32),
            pltpu.VMEM((3 * NODES, WIDTH), bf16),
            pltpu.VMEM((EDGES, HALF), bf16),
            pltpu.VMEM((EDGES, WIDTH), f32),
            pltpu.VMEM((EDGES, 1), f32),
            pltpu.VMEM((NODES, WIDTH), f32),
            pltpu.VMEM((2, NODES, WIDTH), bf16),
            pltpu.VMEM((NODES, WIDTH), bf16),
            pltpu.VMEM((NODES, WIDTH), bf16),
            pltpu.VMEM((EDGES, WIDTH), bf16),
            pltpu.VMEM((EDGES, HALF), bf16),
            pltpu.VMEM((8, WIDTH), f32),
            dma((5,)),
            dma((2, 5)),
        ],
        compiler_params=pltpu.CompilerParams(
            collective_id=0, has_side_effects=True, vmem_limit_bytes=40 * 2**20
        ),
        name="layer",
    )(*operands)


def reduce_kernel(
    g,
    listed,
    edge_mine,
    edge_send,
    table_mine,
    table_send,
    out,
    other,
    grad_nodes,
    grad_edges,
    edge_got,
    table_got,
    table_sum,
    leaving,
    arriving,
    held_wide,
    made_wide,
    kept_wide,
    held_narrow,
    made_narrow,
    kept_narrow,
    held_z,
    sems_wide,
    sems_narrow,
    sems_z,
    sems_out_z,
    sems_out_narrow,
    sems_out_wide,
    sems_core,
    sems_side,
):
    batch = lax.axis_index("batch")
    space = lax.axis_index("space")
    core = lax.axis_index("hidden")
    x = space // 16
    y = (space // 8) % 2 * 2 + batch
    z = space % 8

    def device(i, j, k):
        return (j % 2, (i * 2 + j // 2) * 8 + k, core)

    x_up, x_down = (device((x + k) % 4, y, z) for k in (1, 3))
    y_up, y_down = (device(x, (y + k) % 4, z) for k in (1, 3))
    z_peers = [device(x, y, (z + k) % 8) for k in range(1, 8)]
    _, partner, before, after = places()
    barrier = pltpu.get_barrier_semaphore()
    peers = [x_up, x_down, y_up, y_down, *z_peers, partner, before, after]
    for peer in peers:
        pl.semaphore_signal(barrier, inc=1, device_id=peer, device_id_type=MESH)
    pl.semaphore_wait(barrier, len(peers))

    side = [
        remote(table_send, table_got, sems_side, 0, partner),
        remote(edge_send, edge_got, sems_side, 1, partner),
    ]
    for c in side:
        c.start()
    along = ((x, x_up, x_down), (y, y_up, y_down))
    started = []
    for color in (0, 1):
        pos, ahead, behind = along[color]
        started.append(
            scatter_start(
                g, color * COLOR, WIDE, pos, ahead, behind, held_wide.at[color], sems_wide.at[color]
            )
        )
    side[0].wait_recv()
    table_sum[...] = table_mine[...] + table_got[...].astype(jnp.float32)
    leaving[...] = table_sum[NODES:].astype(jnp.bfloat16)
    side += [
        remote(leaving.at[pl.ds(0, HALO)], arriving.at[pl.ds(HALO, HALO)], sems_side, 2, before),
        remote(leaving.at[pl.ds(HALO, HALO)], arriving.at[pl.ds(0, HALO)], sems_side, 3, after),
    ]
    for c in side[2:]:
        c.start()
    side[1].wait_recv()
    grad_edges[...] = (edge_mine[...] + edge_got[...].astype(jnp.float32)).astype(jnp.bfloat16)
    for color in (0, 1):
        pos, ahead, behind = along[color]
        scatter_middle(
            g, color * COLOR, WIDE, pos, ahead, behind, held_wide.at[color],
            made_wide.at[color], sems_wide.at[color], started[color],
        )
    second = []
    for color in (0, 1):
        pos, ahead, behind = along[color]
        scatter_end(
            g, color * COLOR, WIDE, pos, held_wide.at[color], kept_wide.at[color], 0, started[color]
        )
        pos, ahead, behind = along[1 - color]
        second.append(
            scatter_start(
                kept_wide.at[color], 0, NARROW, pos, ahead, behind,
                held_narrow.at[color], sems_narrow.at[color],
            )
        )
    for c in side[2:]:
        c.wait_recv()
    grad_nodes[...] = (
        table_sum[0:NODES] + nn(hot_columns(listed[...], NODES), arriving[...])
    ).astype(jnp.bfloat16)
    for c in side:
        c.wait_send()
    for color in (0, 1):
        pos, ahead, behind = along[1 - color]
        scatter_middle(
            kept_wide.at[color], 0, NARROW, pos, ahead, behind, held_narrow.at[color],
            made_narrow.at[color], sems_narrow.at[color], second[color],
        )
    for color in (0, 1):
        pos, ahead, behind = along[1 - color]
        scatter_end(
            kept_wide.at[color], 0, NARROW, pos, held_narrow.at[color],
            kept_narrow, color * NARROW, second[color],
        )
    third = []
    for k in range(1, 8):
        c = remote(
            rows_at(kept_narrow, (z + k) % 8 * ZROWS, ZROWS), held_z.at[k - 1], sems_z, k - 1,
            z_peers[k - 1],
        )
        c.start()
        third.append(c)
    total = load_rows(kept_narrow, z * ZROWS, ZROWS)
    for k in range(7):
        third[k].wait_recv()
        total = total + held_z[k].astype(jnp.float32)
    base = (x * WIDE + y * NARROW, COLOR + y * WIDE + x * NARROW)
    upper = z // 4
    mine = (1 - upper) * base[0] + upper * base[1] + z % 4 * ZROWS
    out[pl.ds(pl.multiple_of(mine, 16), ZROWS), :] = total.astype(jnp.bfloat16)
    for c in third:
        c.wait_send()
    third = []
    for k in range(1, 8):
        c = remote(rows_at(out, mine, ZROWS), rows_at(out, mine, ZROWS), sems_out_z, k - 1, z_peers[k - 1])
        c.start()
        third.append(c)
    for c in third:
        c.wait_recv()
    for c in third:
        c.wait_send()
    bases = ((0 + x * WIDE), (COLOR + y * WIDE))
    copies = []
    for color in (0, 1):
        pos, ahead, behind = along[1 - color]
        copies.append(gather_start(out, bases[color], NARROW, pos, ahead, behind, sems_out_narrow.at[color]))
    for color in (0, 1):
        pos, ahead, behind = along[1 - color]
        gather_middle(out, bases[color], NARROW, pos, ahead, behind, sems_out_narrow.at[color], copies[color])
    wide = []
    for color in (0, 1):
        gather_end(copies[color])
        pos, ahead, behind = along[color]
        wide.append(gather_start(out, color * COLOR, WIDE, pos, ahead, behind, sems_out_wide.at[color]))
    for color in (0, 1):
        pos, ahead, behind = along[color]
        gather_middle(out, color * COLOR, WIDE, pos, ahead, behind, sems_out_wide.at[color], wide[color])
    for color in (1, 0):
        gather_end(wide[color])
        if color == 1:
            c = remote(out.at[pl.ds(NODE_AT, NODE_ROWS)], other, sems_core, 0, partner)
            c.start()
    c.wait()


def reduce_call(packed, listed, edge_mine, edge_send, table_mine, table_send):
    dma = pltpu.SemaphoreType.DMA
    bf16, f32 = jnp.bfloat16, jnp.float32
    columns = packed.shape[1]
    vmem = pl.BlockSpec(memory_space=pltpu.VMEM)
    return pl.pallas_call(
        reduce_kernel,
        out_shape=(
            jax.ShapeDtypeStruct(packed.shape, bf16),
            jax.ShapeDtypeStruct((NODE_ROWS, columns), bf16),
            jax.ShapeDtypeStruct((NODES, HALF), bf16),
            jax.ShapeDtypeStruct((EDGES, HALF), bf16),
        ),
        in_specs=[vmem] * 6,
        out_specs=(vmem,) * 4,
        scratch_shapes=[
            pltpu.VMEM((EDGES, HALF), bf16),
            pltpu.VMEM((2 * NODES, HALF), bf16),
            pltpu.VMEM((2 * NODES, HALF), f32),
            pltpu.VMEM((NODES, HALF), bf16),
            pltpu.VMEM((NODES, HALF), bf16),
            pltpu.VMEM((2, 6, WIDE // 2, columns), bf16),
            pltpu.VMEM((2, 2, WIDE // 2, columns), bf16),
            pltpu.VMEM((2, WIDE, columns), bf16),
            pltpu.VMEM((2, 6, NARROW // 2, columns), bf16),
            pltpu.VMEM((2, 2, NARROW // 2, columns), bf16),
            pltpu.VMEM((2 * NARROW, columns), bf16),
            pltpu.VMEM((7, ZROWS, columns), bf16),
            dma((2, 2, 6)),
            dma((2, 2, 6)),
            dma((2, 7)),
            dma((2, 7)),
            dma((2, 2, 6)),
            dma((2, 2, 6)),
            dma((2, 1)),
            dma((2, 4)),
        ],
        compiler_params=pltpu.CompilerParams(
            collective_id=1, has_side_effects=True, vmem_limit_bytes=32 * 2**20
        ),
        name="reduce_all",
    )(packed, listed, edge_mine, edge_send, table_mine, table_send)


def unpack_kernel(
    summed, other, edge_first, edge_bias, edge_second, edge_gain, node_first, node_bias,
    node_second, node_gain,
):
    f32 = jnp.float32
    core = lax.axis_index("hidden")
    edge_first[0:768] = summed[0:768, 0:HALF].astype(f32)
    edge_first[768:1536] = summed[0:768, HALF:].astype(f32)
    edge_second[...] = summed[768:1024].astype(f32)
    small = summed[1792:1808].astype(f32)
    far_small = other[768:784].astype(f32)
    edge_bias[...] = small[0:1, 0:HALF]
    for rows, at, source, values in (
        (core, 1024, summed, small),
        (1 - core, 0, other, far_small),
    ):
        node_first[pl.ds(pl.multiple_of(rows * 512, 512), 512), :] = source[at : at + 512].astype(f32)
        node_second[pl.ds(pl.multiple_of(rows * 256, 256), 256), :] = source[
            at + 512 : at + 768
        ].astype(f32)
        columns = pl.ds(pl.multiple_of(rows * HALF, HALF), HALF)
        edge_gain[:, columns] = values[0:1, HALF:]
        node_bias[:, columns] = values[1:2, 0:HALF]
        node_gain[:, columns] = values[1:2, HALF:]


def unpack_call(summed, other):
    f32 = jnp.float32
    vmem = pl.BlockSpec(memory_space=pltpu.VMEM)
    shapes = ((1536, 256), (1, 256), (256, 512), (1, 512), (1024, 512), (1, 512), (512, 512), (1, 512))
    return pl.pallas_call(
        unpack_kernel,
        out_shape=tuple(jax.ShapeDtypeStruct(shape, f32) for shape in shapes),
        in_specs=[vmem] * 2,
        out_specs=(vmem,) * 8,
        compiler_params=pltpu.CompilerParams(vmem_limit_bytes=32 * 2**20),
        name="unpack",
    )(summed, other)


def on_device(
    nodes,
    edges,
    node_cotangent,
    edge_cotangent,
    senders,
    receivers,
    send_lists,
    edge_first,
    edge_bias,
    edge_second,
    edge_gain,
    node_first,
    node_bias,
    node_second,
    node_gain,
):
    listed = send_lists.reshape(1, -1)
    packed, edge_mine, edge_send, table_mine, table_send = layer_call(
        nodes[0],
        listed,
        senders[None],
        receivers[None],
        edge_first,
        edge_second,
        edge_bias[None],
        edge_gain[None],
        node_bias[None],
        node_gain[None],
        edges[0],
        edge_cotangent[0],
        node_cotangent[0],
        node_first,
        node_second,
    )
    summed, other, grad_nodes, grad_edges = reduce_call(
        packed, listed, edge_mine, edge_send, table_mine, table_send
    )
    first, bias, second, gain, n_first, n_bias, n_second, n_gain = unpack_call(summed, other)
    return (
        grad_nodes[None],
        grad_edges[None],
        first,
        bias[0],
        second,
        gain[0],
        n_first,
        n_bias[0],
        n_second,
        n_gain[0],
    )


def solution(mesh):
    placed = (
        P("batch", "space", None),
        P("batch", "space", None),
        P("batch", "space", None),
        P("batch", "space", None),
        P("space"),
        P("space"),
        P("space", None, None),
        P(None, "hidden"),
        P("hidden"),
        P("hidden", None),
        P(),
        P(),
        P(),
        P(),
        P(),
    )
    return jax.shard_map(
        on_device,
        mesh=mesh,
        in_specs=placed,
        out_specs=(
            P("batch", "space", "hidden"),
            P("batch", "space", "hidden"),
            P(None, "hidden"),
            P("hidden"),
            P("hidden", None),
            P(),
            P(),
            P(),
            P(),
            P(),
        ),
        check_vma=False,
    )
```

time: 138 us -> 101 us (0.73)
  Pallas kernels: 54.1 us -> 84.7 us
  starting transfers between devices: 18.4 us -> 0 us
  matrix products: 17.9 us -> 0 us
  other arithmetic: 14.7 us -> 0 us
  blocking collectives: 10.6 us -> 0 us
  local copies, waits for them, and re-layouts: 20.3 us -> 14.9 us
    pallas_call x1 -> x3, Pallas kernels: 54.1 us -> 84.7 us  [the longest x1 56.8 us: reduce_call(): pl.pallas_call(reduce_kernel, out_shape=(jax.ShapeDtypeStruct(packed.shap...]
    ppermute x4 -> x0, starting transfers between devices: 18.4 us -> none  [the longest x2 15.9 us: extended(): lax.ppermute(head, axis, [((i + 1) % count, i) for i in range(count)])]
    dot_general x20 -> x0, matrix products: 17.9 us -> none  [the longest x8 7.86 us: matmul(): return jnp.dot(lefthand, righthand, preferred_element_type=jnp.float32)]
    all_to_all x2 -> x0, blocking collectives: 10.6 us -> none  [the longest x1 5.99 us: copy_for_each(): lax.all_to_all(jnp.broadcast_to(value[None], (devices, *value.shape)), ax...]
    convert_element_type x8 -> x0, other arithmetic: 9.7 us -> none  [the longest x1 1.8 us: on_device(): edge_second_grad = summed[768:1024].astype(f32)]
    slice x11 -> x0, local copies, waits for them, and re-layouts: 3.3 us -> none  [the longest x1 1.17 us: on_device(): summed[:first_rows, :256]]
    unnamed x60 -> x30, local copies, waits for them, and re-layouts: 11.2 us -> 14.1 us
    dynamic_slice x2 -> x0, local copies, waits for them, and re-layouts: 2.62 us -> none  [on_device(): lax.dynamic_slice_in_dim(edge_upstream, my_part * half, half, 1)]
  transfers between devices with their start and end apart: 4 -> 0, of which waited for: 0 -> 0; matrix products, arithmetic and copies ran while one was open for 10% -> 0% of each run, Pallas kernels for 0% -> 0%
where the time goes in v2:
time: 101 us; the launch traced here: 100 us
  Pallas kernels  84.7 us (84%)
  local copies, waits for them, and re-layouts  14.9 us (15%)
    pallas_call x1, Pallas kernels, reduce_call(): pl.pallas_call(reduce_kernel, out_shape=(jax.ShapeDtypeStruct(packed.shap...  56.8 us
    pallas_call x1, Pallas kernels, layer_call(): pl.pallas_call(layer_kernel, out_shape=(jax.ShapeDtypeStruct((ROWS, WIDTH...  25.3 us
    unnamed x30, local copies, waits for them, and re-layouts  14.1 us
    pallas_call x1, Pallas kernels, unpack_call(): pl.pallas_call(unpack_kernel, out_shape=tuple((jax.ShapeDtypeStruct(shape...  2.57 us

profile of v2, /device:TPU:1, one launch (start us, length us, event | category | flops | bytes accessed | tf_op | source)
XLA Modules:
  0.0 100.3 jit_solution(2109630609794249022)
XLA Ops:
  0.6 0.8 reshape.23.listed
  1.4 0.0 copy-start
  1.4 1.2 %copy-done = bf16[1,1024,512]{2,1,0:T(8,128)(2,1)S(1)} copy-done((bf16[1,1024,512]{2,1,0:T(8,128)(2,1)S(1)}, bf16[1,1024,512]{2,1,0:T(8,128)(2,1)}, u32[]{:S(2)}) %copy-start) | copy-done | bytes 1048600
  2.6 0.0 copy-start.1
  2.6 1.2 %copy-done.1 = bf16[1,1024,512]{2,1,0:T(8,128)(2,1)S(1)} copy-done((bf16[1,1024,512]{2,1,0:T(8,128)(2,1)S(1)}, bf16[1,1024,512]{2,1,0:T(8,128)(2,1)}, u32[]{:S(2)}) %copy-start.1) | copy-done | bytes 1048600
  3.9 0.0 copy-start.2
  3.9 1.2 %copy-done.2 = bf16[1024,512]{1,0:T(8,128)(2,1)S(1)} copy-done((bf16[1024,512]{1,0:T(8,128)(2,1)S(1)}, bf16[1024,512]{1,0:T(8,128)(2,1)}, u32[]{:S(2)}) %copy-start.2) | copy-done | bytes 1048600
  5.1 0.0 copy-start.3
  5.1 1.1 %copy-done.3 = bf16[1536,256]{1,0:T(8,128)(2,1)S(1)} copy-done((bf16[1536,256]{1,0:T(8,128)(2,1)S(1)}, bf16[1536,256]{1,0:T(8,128)(2,1)}, u32[]{:S(2)}) %copy-start.3) | copy-done | bytes 786456
  6.2 0.0 copy-start.4
  6.2 1.0 %copy-done.4 = bf16[512,512]{1,0:T(8,128)(2,1)S(1)} copy-done((bf16[512,512]{1,0:T(8,128)(2,1)S(1)}, bf16[512,512]{1,0:T(8,128)(2,1)}, u32[]{:S(2)}) %copy-start.4) | copy-done | bytes 524312
  7.3 0.0 copy-start.5
  7.3 0.9 copy-done.5
  8.2 0.0 copy-start.6
  8.2 0.9 copy-done.6
  9.1 0.0 copy-start.7
  9.1 0.9 copy-done.7
  10.0 0.0 copy-start.8
  10.0 0.7 copy-done.8
  10.7 0.0 copy-start.9
  10.7 0.7 copy-done.9
  11.4 0.0 copy-start.10
  11.4 0.7 copy-done.10
  12.1 0.0 copy-start.11
  12.1 0.7 copy-done.11
  12.8 0.0 copy-start.12
  12.8 0.7 copy-done.12
  13.4 0.0 copy-start.13
  13.4 0.7 copy-done.13
  14.1 25.3 %layer.1 = (bf16[2048,512]{1,0:T(8,128)(2,1)S(1)}, f32[1024,256]{1,0:T(8,128)S(1)}, bf16[1024,256]{1,0:T(8,128)(2,1)S(1)}, f32[256,256]{1,0:T(8,128)S(1)}, bf16[256,256]{1,0:T(8,128)(2,1)S(1)}) custom-call(bf16[128,512]{1,0:T(8,128)(2,1)S(1)} %bitcast.19, s32[1,128]{1,0:T(1,128)S(1)} %reshape.23.listed, s32[1,1024]{1,0:T(1,128)S(1)} %bitcast.22, ...), custom_call_target="tpu_custom_call" | custom-call | tf_op jit(solution)/shard_map/layer/pallas_call | solution.py:377
  39.4 56.8 %reduce_all.1 = (bf16[2048,512]{1,0:T(8,128)(2,1)S(1)}, bf16[784,512]{1,0:T(8,128)(2,1)S(1)}, bf16[128,256]{1,0:T(8,128)(2,1)S(1)}, bf16[1024,256]{1,0:T(8,128)(2,1)S(1)}) custom-call(bf16[2048,512]{1,0:T(8,128)(2,1)S(1)} %get-tuple-element.27.g, s32[1,128]{1,0:T(1,128)S(1)} %reshape.23.listed, f32[1024,256]{1,0:T(8,128)S(1)} %get-tuple-element.28.edge_mine, ...), custom_call_target="tpu_custom_call" | custom-call | tf_op jit(solution)/shard_map/reduce_all/pallas_call | solution.py:594
  96.3 2.6 %unpack.1 = (f32[1536,256]{1,0:T(8,128)}, f32[1,256]{1,0:T(1,128)}, f32[256,512]{1,0:T(8,128)}, f32[1,512]{1,0:T(1,128)}, f32[1024,512]{1,0:T(8,128)}, /*index=5...) custom-call(bf16[2048,512]{1,0:T(8,128)(2,1)S(1)} %get-tuple-element.34.summed, ...), custom_call_target="tpu_custom_call" | custom-call | tf_op jit(solution)/shard_map/unpack/pallas_call | solution.py:663
  98.8 0.6 copy.27
  99.5 0.8 copy.28
Async XLA Ops:
  1.4 1.2 %copy-start = (bf16[1,1024,512]{2,1,0:T(8,128)(2,1)S(1)}, bf16[1,1024,512]{2,1,0:T(8,128)(2,1)}, u32[]{:S(2)}) copy-start(bf16[1,1024,512]{2,1,0:T(8,128)(2,1)} %param.16) | copy-start | bytes 3145732
  2.6 1.2 %copy-start.1 = (bf16[1,1024,512]{2,1,0:T(8,128)(2,1)S(1)}, bf16[1,1024,512]{2,1,0:T(8,128)(2,1)}, u32[]{:S(2)}) copy-start(bf16[1,1024,512]{2,1,0:T(8,128)(2,1)} %param.18) | copy-start | bytes 3145732
  3.9 1.2 %copy-start.2 = (bf16[1024,512]{1,0:T(8,128)(2,1)S(1)}, bf16[1024,512]{1,0:T(8,128)(2,1)}, u32[]{:S(2)}) copy-start(bf16[1024,512]{1,0:T(8,128)(2,1)} %node_first_far.1) | copy-start | bytes 3145732
  5.1 1.1 %copy-start.3 = (bf16[1536,256]{1,0:T(8,128)(2,1)S(1)}, bf16[1536,256]{1,0:T(8,128)(2,1)}, u32[]{:S(2)}) copy-start(bf16[1536,256]{1,0:T(8,128)(2,1)} %first.1) | copy-start | bytes 2359300
  6.2 1.0 %copy-start.4 = (bf16[512,512]{1,0:T(8,128)(2,1)S(1)}, bf16[512,512]{1,0:T(8,128)(2,1)}, u32[]{:S(2)}) copy-start(bf16[512,512]{1,0:T(8,128)(2,1)} %node_second_far.1) | copy-start | bytes 1572868
  7.3 0.9 copy-start.5
  8.2 0.9 copy-start.6
  9.1 0.9 copy-start.7
  10.0 0.7 copy-start.8
  10.7 0.7 copy-start.9
  11.4 0.7 copy-start.10
  12.1 0.7 copy-start.11
  12.8 0.7 copy-start.12
  13.4 0.7 copy-start.13
